TPU v7x, 32 devices: a whole 2x2x4 slice. The times are simulated.
32 devices in a mesh: blocks: 16 (over z, y, x), cross: 2 (over core).
Axes of the slice: x: 2, y: 2, z: 4, core: 2. Of those that a mesh axis runs over, the one named last changes fastest.
Arguments:
- f_home: float32 [1024, 19, 512], P(('blocks', 'cross')), may hold values from -0.5 to 1.5
- levels: int32 [1024], P(('blocks', 'cross')), may hold values from 0 to 1, as said below
- plan: int32 [1024], P(('blocks', 'cross')), may hold values from 0 to 1023, as said below
Outputs:
- f_owner: float32 [1024, 19, 512], P(('blocks', 'cross'))
Inputs may be any that keep to these rules, and one draw needn't show every extreme that they name: `levels`: exactly a quarter of the patches, 8 times the number of devices, have level 1. plan is a permutation of the patch numbers. Of the patches in the slots of one device of f_home, at most 2 have owner slots on one device, and in every draw some device sends exactly 2 to one owner; every device's owner slots receive exactly 8 patches of level 1.
All inputs are finite; a program needn't handle non-finite values.
Results may differ from a plain program's by a relative error of at most 0.0001.
Values sent between devices are 32-bit elements; how exact they have to be, the bound alone decides.
A program may use at most 256 MiB of HBM per device.

v0:
```python
import jax
import jax.numpy as jnp
from jax import lax
from jax.sharding import PartitionSpec as P

FLOW_PATCHES = 1
SPAN_PATCHES = 4
DEPTH_PATCHES = 8
EDGE = 8
STEPS = 2
CELLS = 512


VELOCITIES = (
    (0, 0, 0),
    (1, 0, 0),
    (-1, 0, 0),
    (0, 1, 0),
    (0, -1, 0),
    (0, 0, 1),
    (0, 0, -1),
    (1, 1, 0),
    (-1, -1, 0),
    (1, -1, 0),
    (-1, 1, 0),
    (1, 0, 1),
    (-1, 0, -1),
    (1, 0, -1),
    (-1, 0, 1),
    (0, 1, 1),
    (0, -1, -1),
    (0, 1, -1),
    (0, -1, 1),
)
WEIGHTS = (1.0 / 3.0,) + (1.0 / 18.0,) * 6 + (1.0 / 36.0,) * 12
FACE_SPEEDS = (
    (2, 8, 10, 12, 14),
    (1, 7, 9, 11, 13),
    (4, 8, 9, 16, 18),
    (3, 7, 10, 15, 17),
    (6, 12, 13, 16, 17),
    (5, 11, 14, 15, 18),
)
TAU_COARSE = 0.55
TAU_FINE = 2.0 * TAU_COARSE - 0.5
RESCALE = TAU_FINE / (2.0 * TAU_COARSE)
INFLOW = 0.08


def extended_2(cells, sides, width):
    for axis, dim in sides:
        count = lax.axis_size(axis)
        head = lax.slice_in_dim(cells, 0, width, axis=dim)
        tail = lax.slice_in_dim(cells, cells.shape[dim] - width, cells.shape[dim], axis=dim)
        cells = jnp.concatenate(
            [
                lax.ppermute(tail, axis, [(i, (i + 1) % count) for i in range(count)]),
                cells,
                lax.ppermute(head, axis, [((i + 1) % count, i) for i in range(count)]),
            ],
            axis=dim,
        )
    return cells


def moments(field):
    density = jnp.sum(field, axis=1)
    velocity = []
    for axis_id in range(3):
        forward = [speed for speed in range(19) if VELOCITIES[speed][axis_id] == 1]
        backward = [speed for speed in range(19) if VELOCITIES[speed][axis_id] == -1]
        velocity.append(
            (jnp.sum(field[:, forward], axis=1) - jnp.sum(field[:, backward], axis=1)) / density
        )
    return (density, velocity)


def equilibrium(density, velocity, speeds):
    speed_sq = velocity[0] * velocity[0] + velocity[1] * velocity[1] + velocity[2] * velocity[2]
    columns = []
    for speed in speeds:
        step_x, step_y, step_z = VELOCITIES[speed]
        along = step_x * velocity[0] + step_y * velocity[1] + step_z * velocity[2]
        columns.append(
            WEIGHTS[speed] * density * (1.0 + 3.0 * along + 4.5 * along * along - 1.5 * speed_sq)
        )
    return jnp.stack(columns, axis=1)


def collide(field, relax_rate):
    density, velocity = moments(field)
    balance = equilibrium(density, velocity, range(19))
    relaxed = field + relax_rate[:, None, None, None, None] * (balance - field)
    return (relaxed, balance, density, velocity)


def layer(field, face_id):
    picker = [slice(None)] * field.ndim
    picker[2 + face_id // 2] = 0 if face_id % 2 == 0 else field.shape[-1] - 1
    return field[tuple(picker)]


def face_payload(relaxed, balance, send_scale):
    eq_faces = jnp.stack(
        [layer(balance[:, list(FACE_SPEEDS[face_id])], face_id) for face_id in range(6)], axis=1
    )
    out_faces = jnp.stack(
        [layer(relaxed[:, list(FACE_SPEEDS[face_id])], face_id) for face_id in range(6)], axis=1
    )
    return (eq_faces, send_scale[:, None, None, None, None] * (out_faces - eq_faces))


def inflow_column(speeds):
    values = []
    for speed in speeds:
        along = VELOCITIES[speed][0] * INFLOW
        values.append(
            WEIGHTS[speed] * (1.0 + 3.0 * along + 4.5 * along * along - 1.5 * INFLOW * INFLOW)
        )
    return jnp.array(values, jnp.float32)


def framed(center, top_row, bottom_row, left_col, right_col):
    middle = jnp.concatenate([left_col[..., :, None], center, right_col[..., :, None]], axis=-1)
    corner = jnp.zeros(top_row.shape[:-1] + (1,), top_row.dtype)
    upper = jnp.concatenate([corner, top_row, corner], axis=-1)[..., None, :]
    lower = jnp.concatenate([corner, bottom_row, corner], axis=-1)[..., None, :]
    return jnp.concatenate([upper, middle, lower], axis=-2)


def bordered(center, left_col, right_col):
    return jnp.concatenate([left_col[..., None], center, right_col[..., None]], axis=-1)


def assemble(eq_ext, neq_ext, recv_scale, inflow_side, outflow_side):
    size_x, size_y, size_z = recv_scale.shape
    factor = recv_scale[:, :, :, None, None, None]

    def neighbour(shift_x, shift_y, shift_z, face_id):
        window = (
            slice(1 + shift_x, 1 + shift_x + size_x),
            slice(1 + shift_y, 1 + shift_y + size_y),
            slice(1 + shift_z, 1 + shift_z + size_z),
            face_id,
        )
        return eq_ext[window] + factor * neq_ext[window]

    plane_west = framed(
        neighbour(-1, 0, 0, 1),
        neighbour(-1, -1, 0, 1)[..., -1, :],
        neighbour(-1, 1, 0, 1)[..., 0, :],
        neighbour(-1, 0, -1, 1)[..., :, -1],
        neighbour(-1, 0, 1, 1)[..., :, 0],
    )
    plane_east = framed(
        neighbour(1, 0, 0, 0),
        neighbour(1, -1, 0, 0)[..., -1, :],
        neighbour(1, 1, 0, 0)[..., 0, :],
        neighbour(1, 0, -1, 0)[..., :, -1],
        neighbour(1, 0, 1, 0)[..., :, 0],
    )
    plane_south = bordered(
        neighbour(0, -1, 0, 3),
        neighbour(0, -1, -1, 3)[..., :, -1],
        neighbour(0, -1, 1, 3)[..., :, 0],
    )
    plane_north = bordered(
        neighbour(0, 1, 0, 2), neighbour(0, 1, -1, 2)[..., :, -1], neighbour(0, 1, 1, 2)[..., :, 0]
    )
    plane_below = neighbour(0, 0, -1, 5)
    plane_above = neighbour(0, 0, 1, 4)
    plane_west = jnp.where(
        inflow_side[:, None, None, None, None, None],
        inflow_column(FACE_SPEEDS[1])[:, None, None],
        plane_west,
    )
    plane_east = jnp.where(
        outflow_side[:, None, None, None, None, None],
        inflow_column(FACE_SPEEDS[0])[:, None, None],
        plane_east,
    )
    return (plane_west, plane_east, plane_south, plane_north, plane_below, plane_above)


def propagate(relaxed, planes):
    extent = relaxed.shape[-1]
    padded = jnp.pad(relaxed, ((0, 0), (0, 0), (1, 1), (1, 1), (1, 1)))
    plane_west, plane_east, plane_south, plane_north, plane_below, plane_above = planes
    for column, speed in enumerate(FACE_SPEEDS[1]):
        padded = padded.at[:, speed, 0, :, :].set(plane_west[:, column])
    for column, speed in enumerate(FACE_SPEEDS[0]):
        padded = padded.at[:, speed, extent + 1, :, :].set(plane_east[:, column])
    for column, speed in enumerate(FACE_SPEEDS[3]):
        padded = padded.at[:, speed, 1 : extent + 1, 0, :].set(plane_south[:, column])
    for column, speed in enumerate(FACE_SPEEDS[2]):
        padded = padded.at[:, speed, 1 : extent + 1, extent + 1, :].set(plane_north[:, column])
    for column, speed in enumerate(FACE_SPEEDS[5]):
        padded = padded.at[:, speed, 1 : extent + 1, 1 : extent + 1, 0].set(plane_below[:, column])
    for column, speed in enumerate(FACE_SPEEDS[4]):
        padded = padded.at[:, speed, 1 : extent + 1, 1 : extent + 1, extent + 1].set(
            plane_above[:, column]
        )
    shifted = []
    for speed in range(19):
        step_x, step_y, step_z = VELOCITIES[speed]
        shifted.append(
            padded[
                :,
                speed,
                1 - step_x : 1 - step_x + extent,
                1 - step_y : 1 - step_y + extent,
                1 - step_z : 1 - step_z + extent,
            ]
        )
    return jnp.stack(shifted, axis=1)


def wrap_axis(values, axis_id):
    length = values.shape[axis_id]
    return jnp.concatenate(
        [
            lax.slice_in_dim(values, length - 1, length, axis=axis_id),
            values,
            lax.slice_in_dim(values, 0, 1, axis=axis_id),
        ],
        axis=axis_id,
    )


def pair_slots(target_dev):
    patch_total = target_dev.shape[0]
    order = jnp.arange(patch_total, dtype=jnp.int32)
    earlier = (target_dev[:, None] == target_dev[None, :]) & (order[None, :] < order[:, None])
    return jnp.sum(earlier.astype(jnp.int32), axis=1)


def pack(payload, target_dev, pair_slot, devices, capacity):
    buffer = jnp.zeros((devices, capacity) + payload.shape[1:], payload.dtype)
    return buffer.at[target_dev, pair_slot].set(payload)


def migrate(populations, levels, plan, target_dev, pair_slot, devices, capacity):
    patch_total = populations.shape[0]
    metadata = jnp.stack([plan % patch_total + 1, levels], axis=1)
    recv_state, recv_meta = (
        lax.all_to_all(
            pack(populations, target_dev, pair_slot, devices, capacity),
            ("blocks", "cross"),
            split_axis=0,
            concat_axis=0,
            tiled=True,
        ),
        lax.all_to_all(
            pack(metadata, target_dev, pair_slot, devices, capacity),
            ("blocks", "cross"),
            split_axis=0,
            concat_axis=0,
            tiled=True,
        ),
    )
    total = devices * capacity
    flat_meta = recv_meta.reshape(total, 2)
    target = jnp.where(flat_meta[:, 0] > 0, flat_meta[:, 0] - 1, patch_total)
    anchor = jnp.arange(total, dtype=jnp.int32)
    moved = (
        jnp.zeros(populations.shape, populations.dtype)
        .at[target]
        .set(recv_state.reshape((total,) + populations.shape[1:]), mode="drop")
    )
    owner_levels = jnp.zeros((patch_total,), jnp.int32).at[target].set(flat_meta[:, 1], mode="drop")
    source_dev = (
        jnp.zeros((patch_total,), jnp.int32).at[target].set(anchor // capacity, mode="drop")
    )
    source_pair = (
        jnp.zeros((patch_total,), jnp.int32).at[target].set(anchor % capacity, mode="drop")
    )
    return (moved, owner_levels, source_dev, source_pair)


def home_ghosts(eq_faces, neq_faces, home_levels):
    lattice_shape = (FLOW_PATCHES, SPAN_PATCHES, DEPTH_PATCHES)
    patch_total = eq_faces.shape[0]
    stacked = jnp.stack([eq_faces, neq_faces], axis=1).reshape(lattice_shape + (-1,))
    extended = extended_2(stacked, (("blocks", 0), ("cross", 1)), 1)
    extended = wrap_axis(extended, 2)
    extended = extended.reshape(extended.shape[:3] + (2, 6, 5, EDGE, EDGE))
    recv_scale = (
        jnp.where(home_levels == 1, RESCALE, 1.0).astype(jnp.float32).reshape(lattice_shape)
    )
    span_x = FLOW_PATCHES * lax.axis_size("blocks")
    position = lax.axis_index("blocks") * FLOW_PATCHES + jnp.arange(FLOW_PATCHES, dtype=jnp.int32)
    planes = assemble(
        extended[:, :, :, 0],
        extended[:, :, :, 1],
        recv_scale,
        position == 0,
        position == span_x - 1,
    )
    return tuple((plane.reshape((patch_total,) + plane.shape[3:]) for plane in planes))


def body(f_home, levels, plan):
    devices = lax.axis_size(("blocks", "cross"))
    patch_total = f_home.shape[0]
    capacity = (patch_total + devices - 1) // devices + 1
    target_dev = plan // patch_total
    pair_slot = pair_slots(target_dev)
    send_home = jnp.where(levels == 1, 1.0 / RESCALE, 1.0).astype(jnp.float32)
    cube = (patch_total, 19, EDGE, EDGE, EDGE)
    populations = f_home.reshape(cube)
    fine_mask = levels == 1
    relax_rate = jnp.where(fine_mask, 1.0 / TAU_FINE, 1.0 / TAU_COARSE).astype(jnp.float32)
    fine_rate = jnp.full((patch_total,), 1.0 / TAU_FINE, jnp.float32)
    for round_id in range(STEPS):
        relaxed, balance, density, velocity = collide(populations, relax_rate)
        eq_faces, neq_faces = face_payload(relaxed, balance, send_home)
        planes = home_ghosts(eq_faces, neq_faces, levels)
        populations = propagate(relaxed, planes)
        updated = propagate(collide(populations, fine_rate)[0], planes)
        populations = jnp.where(fine_mask[:, None, None, None, None], updated, populations)
    return migrate(
        populations.reshape(patch_total, 19, CELLS),
        levels,
        plan,
        target_dev,
        pair_slot,
        devices,
        capacity,
    )[0]


def solution(mesh):
    in_specs = (P(("blocks", "cross"), None, None), P(("blocks", "cross")), P(("blocks", "cross")))
    out_specs = P(("blocks", "cross"), None, None)
    return jax.shard_map(body, mesh=mesh, in_specs=in_specs, out_specs=out_specs, check_vma=False)
```

profile of v0, /device:TPU:0, one launch (start us, length us, event | category | flops | bytes accessed | tf_op | source)
XLA Modules:
  0.0 1177.6 jit_solution(14872393180522574223)
XLA Ops:
  65.4 8.0 multiply_add_fusion.3
  104.0 5.2 reshape.9081
  109.3 5.6 copy.987
  122.2 16.7 %collective-permute-done = f32[1,4,8,3840]{3,2,1,0:T(8,128)S(1)} collective-permute-done((f32[1,4,8,3840]{3,2,1,0:T(8,128)S(1)}, f32[1,4,8,3840]{3,2,1,0:T(8,128)S(1)}, u32[]{:S(2)}, u32[]{:S(2)}) %collective-permute-start) | collective-permute-done | bytes 491552 | tf_op jit(solution)/shard_map/ppermute | solution.py:57
  141.5 10.2 pad.493
  156.7 27.5 %reshape.8613 = f32[3,6,10,2,6,5,8,8]{7,6,5,4,3,1,2,0:T(8,128)} reshape(f32[3,6,10,3840]{3,1,2,0:T(8,128)} %copy.787) | data formatting | bytes 5529600 | tf_op jit(solution)/shard_map/reshape | solution.py:286
  184.2 22.4 %slice_bitcast_fusion = (f32[3,6,10,6,5,8,8]{6,5,4,3,1,2,0:T(8,128)}, f32[3,6,10,1,6,5,8,8]{7,6,5,4,3,1,2,0:T(8,128)S(1)}) fusion(f32[3,6,10,2,6,5,8,8]{7,6,5,4,3,1,2,0:T(8,128)} %reshape.8613), kind=kLoop, calls=%fused_computation.51 | loop fusion | bytes 5529600 | tf_op jit(solution)/shard_map/squeeze | solution.py:294
  206.6 7.9 copy.1035
  214.5 8.3 fusion.345
  248.2 9.4 fusion.344
  283.7 6.4 slice_add_fusion.9
  290.2 11.0 copy.822
  436.9 7.7 pad.494
  495.2 5.9 fusion.340
  575.5 8.0 multiply_add_fusion.1
  613.4 5.2 reshape.9082
  618.6 5.7 copy.988
  630.0 17.1 %collective-permute-done.4 = f32[1,4,8,3840]{3,2,1,0:T(8,128)S(1)} collective-permute-done((f32[1,4,8,3840]{3,2,1,0:T(8,128)S(1)}, f32[1,4,8,3840]{3,2,1,0:T(8,128)S(1)}, u32[]{:S(2)}, u32[]{:S(2)}) %collective-permute-start.4) | collective-permute-done | bytes 491552 | tf_op jit(solution)/shard_map/ppermute | solution.py:57
  658.4 10.2 pad.495
  671.4 27.9 %reshape.9083 = f32[3,6,10,2,6,5,8,8]{7,6,5,4,3,2,1,0:T(8,128)} reshape(f32[3,6,10,3840]{3,2,1,0:T(8,128)} %fusion) | data formatting | bytes 5529600 | tf_op jit(solution)/shard_map/reshape | solution.py:286
  699.3 22.5 %fusion.341 = (f32[3,6,10,1,6,5,8,8]{7,6,5,4,3,2,1,0:T(8,128)}, f32[3,6,10,1,6,5,8,8]{7,6,5,4,3,2,1,0:T(8,128)S(1)}) fusion(f32[3,6,10,2,6,5,8,8]{7,6,5,4,3,2,1,0:T(8,128)} %reshape.9083), kind=kLoop, calls=%fused_computation.992 | loop fusion | bytes 5529600 | tf_op jit(solution)/shard_map/slice | solution.py:294
  721.7 7.9 copy.1034
  729.6 8.3 fusion.343
  741.7 17.2 %copy.1033 = f32[3,6,10,1,6,5,8,8]{7,6,5,1,2,4,0,3:T(8,128)} copy(f32[3,6,10,1,6,5,8,8]{7,6,5,4,3,2,1,0:T(8,128)} %get-tuple-element.1465) | data formatting | bytes 2764800
  758.9 9.3 fusion.342
  815.8 6.8 slice_add_fusion.1
  882.8 5.8 fusion.346
  996.3 7.7 pad.496
  1034.5 5.5 fusion.348
  1102.9 5.8 all-to-all-start.1
  1109.5 56.4 %all-to-all-done.1 = f32[32,2,19,512]{3,1,2,0:T(2,128)S(1)} async-done(((f32[32,2,19,512]{3,1,2,0:T(2,128)}), f32[32,2,19,512]{3,1,2,0:T(2,128)S(1)}, u32[]{:S(2)}, u32[]{:S(2)}) %all-to-all-start.1) | async-done | bytes 2490400 | tf_op jit(solution)/shard_map/all_to_all | solution.py:246
  1168.3 7.1 scatter_fusion.2
  (881 shorter events, 787.7 us)
Async XLA Ops:
  4.4 579.1 %copy-start.105 = (s32[1024]{0:T(1024)}, s32[1024]{0:T(1024)S(1)}, u32[]{:S(2)}) copy-start(s32[1024]{0:T(1024)S(1)} %get-tuple-element.1650) | copy-start | bytes 12292
  10.9 70.7 %copy-start.106 = (s32[1024]{0:T(1024)}, s32[1024]{0:T(1024)S(1)}, u32[]{:S(2)}) copy-start(s32[1024]{0:T(1024)S(1)} %get-tuple-element.1648) | copy-start | bytes 12292
  10.9 74.8 %copy-start.108 = (s32[1024]{0:T(1024)}, s32[1024]{0:T(1024)S(1)}, u32[]{:S(2)}) copy-start(s32[1024]{0:T(1024)S(1)} %get-tuple-element.1649) | copy-start | bytes 12292
  17.3 71.4 %copy-start.110 = (s32[1024]{0:T(1024)}, s32[1024]{0:T(1024)S(1)}, u32[]{:S(2)}) copy-start(s32[1024]{0:T(1024)S(1)} %get-tuple-element.1646) | copy-start | bytes 12292
  17.3 74.5 %copy-start.111 = (s32[1024]{0:T(1024)}, s32[1024]{0:T(1024)S(1)}, u32[]{:S(2)}) copy-start(s32[1024]{0:T(1024)S(1)} %get-tuple-element.1647) | copy-start | bytes 12292
  65.4 38.3 %copy-start.113 = (f32[32]{0:T(128)}, f32[32]{0:T(128)S(1)}, u32[]{:S(2)}) copy-start(f32[32]{0:T(128)S(1)} %get-tuple-element.1643) | copy-start | bytes 388
  65.4 86.3 %copy-start.112 = (f32[32]{0:T(128)}, f32[32]{0:T(128)S(1)}, u32[]{:S(2)}) copy-start(f32[32]{0:T(128)S(1)} %get-tuple-element.1641) | copy-start | bytes 388
  114.9 24.0 %collective-permute-start = (f32[1,4,8,3840]{3,2,1,0:T(8,128)S(1)}, f32[1,4,8,3840]{3,2,1,0:T(8,128)S(1)}, u32[]{:S(2)}, u32[]{:S(2)}) collective-permute-start(f32[1,4,8,3840]{3,2,1,0:T(8,128)S(1)} %copy.987), channel_id=1, source_target_pairs={{0,2},{2,4},{4,6},{6,8},{8,10},{10,12},{12,14},{14,16},{16,18},{18... | collective-permute-start | bytes 1474568 | tf_op jit(solution)/shard_map/ppermute | solution.py:57
  117.9 23.0 %collective-permute-start.1 = (f32[1,4,8,3840]{3,2,1,0:T(8,128)S(1)}, f32[1,4,8,3840]{3,2,1,0:T(8,128)S(1)}, u32[]{:S(2)}, u32[]{:S(2)}) collective-permute-start(f32[1,4,8,3840]{3,2,1,0:T(8,128)S(1)} %copy.987), channel_id=1, source_target_pairs={{2,0},{4,2},{6,4},{8,6},{10,8},{12,10},{14,12},{16,14},{18,16},{20... | collective-permute-start | bytes 1474568 | tf_op jit(solution)/shard_map/ppermute | solution.py:59
  140.9 11.5 collective-permute-start.2
  141.0 11.5 collective-permute-start.3
  151.9 163.6 %copy-start.87 = (f32[4,8]{0,1:T(8,128)}, f32[4,8]{0,1:T(8,128)S(1)}, u32[]{:S(2)}) copy-start(f32[4,8]{0,1:T(8,128)S(1)} %copy.789) | copy-start | bytes 388
  290.1 35.3 %copy-start.35 = (f32[32,5,8,8]{0,3,2,1:T(8,128)S(1)}, f32[32,5,8,8]{0,3,2,1:T(8,128)}, u32[]{:S(2)}) copy-start(f32[32,5,8,8]{0,3,2,1:T(8,128)} %squeeze.168) | copy-start | bytes 122884
  290.1 35.3 %copy-start.36 = (f32[32,5,8,8]{0,3,2,1:T(8,128)S(1)}, f32[32,5,8,8]{0,3,2,1:T(8,128)}, u32[]{:S(2)}) copy-start(f32[32,5,8,8]{0,3,2,1:T(8,128)} %squeeze.176) | copy-start | bytes 122884
  290.1 35.3 %copy-start.37 = (f32[32,5,8,8]{0,3,2,1:T(8,128)S(1)}, f32[32,5,8,8]{0,3,2,1:T(8,128)}, u32[]{:S(2)}) copy-start(f32[32,5,8,8]{0,3,2,1:T(8,128)} %squeeze.182) | copy-start | bytes 122884
  290.1 35.3 %copy-start.38 = (f32[32,5,8,8]{0,3,2,1:T(8,128)S(1)}, f32[32,5,8,8]{0,3,2,1:T(8,128)}, u32[]{:S(2)}) copy-start(f32[32,5,8,8]{0,3,2,1:T(8,128)} %squeeze.186) | copy-start | bytes 122884
  290.1 35.3 %copy-start.39 = (f32[32,5,8,8]{0,3,2,1:T(8,128)S(1)}, f32[32,5,8,8]{0,3,2,1:T(8,128)}, u32[]{:S(2)}) copy-start(f32[32,5,8,8]{0,3,2,1:T(8,128)} %squeeze.188) | copy-start | bytes 122884
  290.1 35.3 %copy-start.46 = (f32[32,5,8,8]{0,3,2,1:T(8,128)S(1)}, f32[32,5,8,8]{0,3,2,1:T(8,128)}, u32[]{:S(2)}) copy-start(f32[32,5,8,8]{0,3,2,1:T(8,128)} %squeeze.159) | copy-start | bytes 122884
  341.0 47.6 %copy-start.73 = (f32[32,1,8,8]{0,3,2,1:T(8,128)}, f32[32,1,8,8]{0,3,2,1:T(8,128)S(1)}, u32[]{:S(2)}) copy-start(f32[32,1,8,8]{0,3,2,1:T(8,128)S(1)} %get-tuple-element.1600) | copy-start | bytes 24580
  341.0 47.6 %copy-start.77 = (f32[32,1,8,8]{0,3,2,1:T(8,128)}, f32[32,1,8,8]{0,3,2,1:T(8,128)S(1)}, u32[]{:S(2)}) copy-start(f32[32,1,8,8]{0,3,2,1:T(8,128)S(1)} %get-tuple-element.1601) | copy-start | bytes 24580
  341.0 47.6 %copy-start.79 = (f32[32,1,8,8]{0,3,2,1:T(8,128)}, f32[32,1,8,8]{0,3,2,1:T(8,128)S(1)}, u32[]{:S(2)}) copy-start(f32[32,1,8,8]{0,3,2,1:T(8,128)S(1)} %get-tuple-element.1602) | copy-start | bytes 24580
  341.0 47.6 %copy-start.81 = (f32[32,1,8,8]{0,3,2,1:T(8,128)}, f32[32,1,8,8]{0,3,2,1:T(8,128)S(1)}, u32[]{:S(2)}) copy-start(f32[32,1,8,8]{0,3,2,1:T(8,128)S(1)} %get-tuple-element.1603) | copy-start | bytes 24580
  341.0 47.6 %copy-start.83 = (f32[32,1,8,8]{0,3,2,1:T(8,128)}, f32[32,1,8,8]{0,3,2,1:T(8,128)S(1)}, u32[]{:S(2)}) copy-start(f32[32,1,8,8]{0,3,2,1:T(8,128)S(1)} %get-tuple-element.1604) | copy-start | bytes 24580
  341.1 49.4 %copy-start.71 = (f32[32,1,8,8]{0,3,2,1:T(8,128)}, f32[32,1,8,8]{0,3,2,1:T(8,128)S(1)}, u32[]{:S(2)}) copy-start(f32[32,1,8,8]{0,3,2,1:T(8,128)S(1)} %get-tuple-element.1598) | copy-start | bytes 24580
  341.1 49.4 %copy-start.75 = (f32[32,1,8,8]{0,3,2,1:T(8,128)}, f32[32,1,8,8]{0,3,2,1:T(8,128)S(1)}, u32[]{:S(2)}) copy-start(f32[32,1,8,8]{0,3,2,1:T(8,128)S(1)} %get-tuple-element.1599) | copy-start | bytes 24580
  624.3 22.8 %collective-permute-start.4 = (f32[1,4,8,3840]{3,2,1,0:T(8,128)S(1)}, f32[1,4,8,3840]{3,2,1,0:T(8,128)S(1)}, u32[]{:S(2)}, u32[]{:S(2)}) collective-permute-start(f32[1,4,8,3840]{3,2,1,0:T(8,128)S(1)} %copy.988), channel_id=1, source_target_pairs={{0,2},{2,4},{4,6},{6,8},{8,10},{10,12},{12,14},{14,16},{16,18},{18... | collective-permute-start | bytes 1474568 | tf_op jit(solution)/shard_map/ppermute | solution.py:57
  625.8 23.7 %collective-permute-start.5 = (f32[1,4,8,3840]{3,2,1,0:T(8,128)S(1)}, f32[1,4,8,3840]{3,2,1,0:T(8,128)S(1)}, u32[]{:S(2)}, u32[]{:S(2)}) collective-permute-start(f32[1,4,8,3840]{3,2,1,0:T(8,128)S(1)} %copy.988), channel_id=1, source_target_pairs={{2,0},{4,2},{6,4},{8,6},{10,8},{12,10},{14,12},{16,14},{18,16},{20... | collective-permute-start | bytes 1474568 | tf_op jit(solution)/shard_map/ppermute | solution.py:59
  649.6 19.0 %collective-permute-start.6 = (f32[3,1,8,3840]{3,2,1,0:T(8,128)S(1)}, f32[3,1,8,3840]{3,2,1,0:T(8,128)S(1)}, u32[]{:S(2)}, u32[]{:S(2)}) collective-permute-start(f32[3,1,8,3840]{3,2,1,0:T(8,128)S(1)} %get-tuple-element.1581), channel_id=1, source_target_pairs={{0,1},{1,0},{2,3},{3,2},{4,5},{5,4},{6,7},{7,6},{8,9},{9,8},{10,11... | collective-permute-start | bytes 1105928 | tf_op jit(solution)/shard_map/ppermute | solution.py:57
  649.7 18.9 %collective-permute-start.7 = (f32[3,1,8,3840]{3,2,1,0:T(8,128)S(1)}, f32[3,1,8,3840]{3,2,1,0:T(8,128)S(1)}, u32[]{:S(2)}, u32[]{:S(2)}) collective-permute-start(f32[3,1,8,3840]{3,2,1,0:T(8,128)S(1)} %get-tuple-element.1582), channel_id=1, source_target_pairs={{1,0},{0,1},{3,2},{2,3},{5,4},{4,5},{7,6},{6,7},{9,8},{8,9},{11,10... | collective-permute-start | bytes 1105928 | tf_op jit(solution)/shard_map/ppermute | solution.py:59
  654.7 448.2 %all-to-all-start = ((s32[32,2,2]{2,1,0:T(2,128)}), s32[32,2,2]{2,1,0:T(2,128)}, u32[]{:S(2)}, u32[]{:S(2)}) async-start(s32[32,2,2]{2,1,0:T(2,128)} %scatter_fusion), calls=%async_computation | async-start | bytes 65536 | tf_op jit(solution)/shard_map/all_to_all | solution.py:253
  1044.9 47.6 %copy-start.118 = (pred[32]{0:T(512)(128)(4,1)S(1)}, pred[32]{0:T(512)(128)(4,1)}, u32[]{:S(2)}) copy-start(pred[32]{0:T(512)(128)(4,1)} %broadcast_compare_fusion) | copy-start | bytes 100
  1102.9 63.0 %all-to-all-start.1 = ((f32[32,2,19,512]{3,1,2,0:T(2,128)}), f32[32,2,19,512]{3,1,2,0:T(2,128)S(1)}, u32[]{:S(2)}, u32[]{:S(2)}) async-start(f32[32,2,19,512]{3,1,2,0:T(2,128)} %copy.982), calls=%async_computation.1 | async-start | bytes 4980736 | tf_op jit(solution)/shard_map/all_to_all | solution.py:246
  (106 other events, 1635.2 us)
where the time goes:
time: 1200 us; the launch traced here: 1180 us
  local copies, waits for them, and re-layouts  919 us (77%)
  other arithmetic  137 us (11%)
  waiting for transfers between devices  94.6 us (8%)
  starting transfers between devices  23.6 us (2%)
    unnamed x379, local copies, waits for them, and re-layouts  150 us
    slice x28, local copies, waits for them, and re-layouts, neighbour(): return eq_ext[window] + factor * neq_ext[window]  90 us
    another operation x43, local copies, waits for them, and re-layouts, propagate(): return jnp.stack(shifted, axis=1)  62.5 us
    all_to_all x1, waiting for transfers between devices, migrate(): lax.all_to_all(pack(populations, target_dev, pair_slot, devices, capacity...  56.4 us
    gather x23, local copies, waits for them, and re-layouts, face_payload(): balance[:, list(FACE_SPEEDS[face_id])]  55.4 us
    reshape x2, local copies, waits for them, and re-layouts, home_ghosts(): extended = extended.reshape(extended.shape[:3] + (2, 6, 5, EDGE, EDGE))  55.4 us
    squeeze x24, local copies, waits for them, and re-layouts, neighbour(): return eq_ext[window] + factor * neq_ext[window]  48.1 us
    unnamed x72, other arithmetic  47.8 us
  transfers between devices with their start and end apart: 10, of which 5 were waited for; matrix products, arithmetic and copies ran while one was open for 39% of the time, Pallas kernels for 0%

commit v1 on v0

v1 whole, which is shorter than its diff:
```python
import jax
import jax.numpy as jnp
from jax import lax
from jax.experimental import pallas as pl
from jax.experimental.pallas import tpu as pltpu
from jax.sharding import PartitionSpec as P

SPAN_PATCHES = 4
DEPTH_PATCHES = 8
STEPS = 2
CELLS = 512
VELOCITIES = (
    (0, 0, 0),
    (1, 0, 0),
    (-1, 0, 0),
    (0, 1, 0),
    (0, -1, 0),
    (0, 0, 1),
    (0, 0, -1),
    (1, 1, 0),
    (-1, -1, 0),
    (1, -1, 0),
    (-1, 1, 0),
    (1, 0, 1),
    (-1, 0, -1),
    (1, 0, -1),
    (-1, 0, 1),
    (0, 1, 1),
    (0, -1, -1),
    (0, 1, -1),
    (0, -1, 1),
)
WEIGHTS = (1.0 / 3.0,) + (1.0 / 18.0,) * 6 + (1.0 / 36.0,) * 12
TAU_COARSE = 0.55
TAU_FINE = 2.0 * TAU_COARSE - 0.5
RESCALE = TAU_FINE / (2.0 * TAU_COARSE)
INFLOW = 0.08
MESH = pl.DeviceIdType.MESH
PACK = 40
LANES = 128
TILES = CELLS // LANES
Y_UP = [q for q in range(19) if VELOCITIES[q][1] == 1]
Y_DOWN = [q for q in range(19) if VELOCITIES[q][1] == -1]
X_UP = [q for q in range(19) if VELOCITIES[q][0] == 1]
X_DOWN = [q for q in range(19) if VELOCITIES[q][0] == -1]
AROUND = [(dx, dy) for dx in (-1, 0, 1) for dy in (-1, 0, 1) if (dx, dy) != (0, 0)]


def relax_into(load, store, coef):
    f = [load(q) for q in range(19)]
    rho = f[0]
    for q in range(1, 19):
        rho = rho + f[q]
    inv = 1.0 / rho
    u = []
    for axis in range(3):
        up = [f[q] for q in range(19) if VELOCITIES[q][axis] == 1]
        down = [f[q] for q in range(19) if VELOCITIES[q][axis] == -1]
        total = up[0] - down[0]
        for a, b in zip(up[1:], down[1:]):
            total = total + (a - b)
        u.append(total * inv)
    base = 1.0 - 1.5 * (u[0] * u[0] + u[1] * u[1] + u[2] * u[2])
    scaled = {w: w * rho for w in set(WEIGHTS)}
    for q in range(19):
        along = None
        for axis in range(3):
            e = VELOCITIES[q][axis]
            if e:
                term = u[axis] if e == 1 else -u[axis]
                along = term if along is None else along + term
        poly = base if along is None else base + along * (3.0 + 4.5 * along)
        balance = scaled[WEIGHTS[q]] * poly
        store(q, balance + coef(q) * (f[q] - balance))


def lattice_kernel(nb, nc, sidx, f_ref, lev_ref, meta_ref, out_ref, st, pb, cq, pm, lv, ys, yr, xs, xr,
                   send_sem, recv_sem, lsend, lrecv):
    b = lax.axis_index("blocks")
    c = lax.axis_index("cross")

    def at(dx, dy):
        return (lax.rem(b + dx + nb, nb), lax.rem(c + dy + nc, nc))

    barrier = pltpu.get_barrier_semaphore()
    for dx, dy in AROUND:
        pl.semaphore_signal(barrier, inc=1, device_id=at(dx, dy), device_id_type=MESH)
    pl.semaphore_wait(barrier, len(AROUND))

    level_copies = []
    for n, (dx, dy) in enumerate(AROUND):
        copy = pltpu.make_async_remote_copy(
            src_ref=lev_ref, dst_ref=lv.at[n], send_sem=lsend.at[n], recv_sem=lrecv.at[n],
            device_id=at(-dx, -dy), device_id_type=MESH)
        copy.start()
        level_copies.append(copy)

    for q in range(19):
        for r in range(SPAN_PATCHES):
            st[q, r] = f_ref[r * 8 : r * 8 + 8, q, :]

    for copy in level_copies:
        copy.wait()

    own = lev_ref[...]
    scale = {(0, 0): jnp.where(own > 0.5, RESCALE, 1.0)}
    for n, key in enumerate(AROUND):
        scale[key] = jnp.where(lv[n] > 0.5, RESCALE, 1.0)
    patch_scale = {}
    for dx in (-1, 0, 1):
        patch_scale[dx, 0] = scale[dx, 0]
        patch_scale[dx, 1] = jnp.concatenate([scale[dx, 0][1:], scale[dx, 1][:1]], axis=0)
        patch_scale[dx, -1] = jnp.concatenate([scale[dx, -1][-1:], scale[dx, 0][:-1]], axis=0)
    gain = jnp.where(own > 0.5, (1.0 - 1.0 / TAU_FINE) / RESCALE, 1.0 - 1.0 / TAU_COARSE)

    def target_scale(dx, dy, dz):
        value = patch_scale[dx, dy]
        return pltpu.roll(value, (-dz) % 8, axis=1) if dz else value

    shape = (SPAN_PATCHES, 8, LANES)
    lane = lax.broadcasted_iota(jnp.int32, shape, 2)
    for q in range(1, 19):
        e = VELOCITIES[q]
        kinds = [{}]
        for axis in range(3):
            if e[axis]:
                kinds = [{**k, axis: v} for k in kinds for v in (0, 1)]
        table = [(k, target_scale(*[e[a] * k.get(a, 0) for a in range(3)])) for k in kinds]
        for tile in range(TILES):
            cell = lane + tile * LANES
            coord = (cell // 64, (cell // 8) % 8, cell % 8)
            result = table[0][1]
            for k, value in table[1:]:
                mask = None
                for axis, on in k.items():
                    if on:
                        hit = coord[axis] == (7 if e[axis] == 1 else 0)
                        mask = hit if mask is None else mask & hit
                result = jnp.where(mask, value, result)
            cq[q - 1, :, :, tile * LANES : (tile + 1) * LANES] = gain * result

    full = (SPAN_PATCHES, 8, CELLS)
    cell = lax.broadcasted_iota(jnp.int32, full, 2)
    coord = (cell // 64, (cell // 8) % 8, cell % 8)
    entry = {
        (axis, e): coord[axis] == (0 if e == 1 else 7) for axis in range(3) for e in (1, -1)
    }
    half = lax.broadcasted_iota(jnp.int32, (2, 8, LANES), 2) < 64
    fine = jnp.broadcast_to(own[:, :, :1] > 0.5, full)

    def roll(v, amount):
        return pltpu.roll(v, amount % CELLS, axis=2)

    def step(s, carry):
        def chunk(t, carry):
            r = t // TILES
            lanes = pl.ds(pl.multiple_of(lax.rem(t, TILES) * LANES, LANES), LANES)
            plain = jnp.where(lev_ref[r] > 0.5, 1.0 - 1.0 / TAU_FINE, 1.0 - 1.0 / TAU_COARSE)

            def put(q, value):
                pb[q, r, :, lanes] = value

            relax_into(lambda q: st[q, r, :, lanes], put,
                       lambda q: cq[q - 1, r, :, lanes] if q else plain)
            return carry

        lax.fori_loop(0, SPAN_PATCHES * TILES, chunk, 0)

        for q in range(19):
            e = VELOCITIES[q][2]
            if e:
                v = pb[q]
                wrapped = pltpu.roll(roll(v, e - 8 * e), e % 8, axis=1)
                pb[q] = jnp.where(entry[2, e], wrapped, roll(v, e))
        for n in range(5):
            ys[s, 0, n] = pb[Y_UP[n], SPAN_PATCHES - 1]
            ys[s, 1, n] = pb[Y_DOWN[n], 0]
        y_copies = []
        for way, dy in ((0, 1), (1, -1)):
            copy = pltpu.make_async_remote_copy(
                src_ref=ys.at[s, way], dst_ref=yr.at[s, way], send_sem=send_sem.at[s, way],
                recv_sem=recv_sem.at[s, way], device_id=at(0, dy), device_id_type=MESH)
            copy.start()
            y_copies.append(copy)
        st[0] = pb[0]
        st[5] = pb[5]
        st[6] = pb[6]
        for copy in y_copies:
            copy.wait()
        for way, e, group in ((0, 1, Y_UP), (1, -1, Y_DOWN)):
            for n, q in enumerate(group):
                v = pb[q]
                halo = yr[s, way, n][None]
                if e == 1:
                    moved = jnp.concatenate([halo, v[:-1]], axis=0)
                else:
                    moved = jnp.concatenate([v[1:], halo], axis=0)
                v = jnp.where(entry[1, e], roll(moved, 8 * e - 64 * e), roll(v, 8 * e))
                if VELOCITIES[q][0]:
                    pb[q] = v
                else:
                    st[q] = v
        for way, e, group in ((0, 1, X_UP), (1, -1, X_DOWN)):
            for n, q in enumerate(group):
                v = roll(pb[q], 64 * e)
                pb[q] = v
                edge = v[:, :, :LANES] if e == 1 else v[:, :, CELLS - LANES :]
                turned = pltpu.roll(edge, 64, axis=2)
                if e == 1:
                    xs[s, way, n] = jnp.where(half, edge[:2], turned[2:])
                else:
                    xs[s, way, n] = jnp.where(half, turned[:2], edge[2:])
        x_copies = []
        for way, dx in ((0, 1), (1, -1)):
            copy = pltpu.make_async_remote_copy(
                src_ref=xs.at[s, way], dst_ref=xr.at[s, way], send_sem=send_sem.at[s, 2 + way],
                recv_sem=recv_sem.at[s, 2 + way], device_id=at(dx, 0), device_id_type=MESH)
            copy.start()
            x_copies.append(copy)
        for copy in x_copies:
            copy.wait()
        for way, e, group in ((0, 1, X_UP), (1, -1, X_DOWN)):
            outside = b == (0 if e == 1 else nb - 1)
            for n, q in enumerate(group):
                h = xr[s, way, n]
                turned = pltpu.roll(h, 64, axis=2)
                halo = jnp.concatenate([h, turned] if e == 1 else [turned, h], axis=0)
                along = e * INFLOW
                const = WEIGHTS[q] * (1.0 + 3.0 * along + 4.5 * along * along - 1.5 * INFLOW * INFLOW)
                halo = jnp.where(outside, jnp.full(halo.shape, const, jnp.float32), halo)
                if e == 1:
                    st[q, :, :, LANES:] = pb[q, :, :, LANES:]
                    st[q, :, :, :LANES] = jnp.where(lane < 64, halo, pb[q, :, :, :LANES])
                else:
                    st[q, :, :, : CELLS - LANES] = pb[q, :, :, : CELLS - LANES]
                    st[q, :, :, CELLS - LANES :] = jnp.where(lane >= 64, halo, pb[q, :, :, CELLS - LANES :])

        def again(t, carry):
            r = t // TILES
            lanes = pl.ds(pl.multiple_of(lax.rem(t, TILES) * LANES, LANES), LANES)

            def put(q, value):
                pb[q, r, :, lanes] = value

            relax_into(lambda q: st[q, r, :, lanes], put, lambda q: 1.0 - 1.0 / TAU_FINE)
            return carry

        lax.fori_loop(0, SPAN_PATCHES * TILES, again, 0)
        for q in range(19):
            e = VELOCITIES[q]
            take = fine
            for axis in range(3):
                if e[axis]:
                    take = take & ~entry[axis, e[axis]]
            moved = pb[q]
            if q:
                moved = roll(moved, 64 * e[0] + 8 * e[1] + e[2])
            st[q] = jnp.where(take, moved, st[q])
        return carry

    lax.fori_loop(0, STEPS, step, 0)

    for q in range(19):
        for r in range(SPAN_PATCHES):
            pm[r * 8 : r * 8 + 8, q, :] = st[q, r]

    def fill(d, carry):
        for slot in range(2):
            p = sidx[2 * d + slot]
            out_ref[d, 16 * slot : 16 * slot + 16, :] = pm[p, :16, :]
            out_ref[d, 32 + 4 * slot : 35 + 4 * slot, :] = pm[p, 16:19, :]
            out_ref[d, 35 + 4 * slot, :] = meta_ref[d, slot, :]
        return carry

    lax.fori_loop(0, nb * nc, fill, 0)


def unpack_kernel(ridx, got_ref, out_ref):
    def place(t, carry):
        a = ridx[t]
        src = a // 2
        slot = lax.rem(a, 2)
        out_ref[t, :16, :] = got_ref[src, pl.ds(pl.multiple_of(slot * 16, 16), 16), :]
        tail = got_ref[src, 32:40, :]
        out_ref[t, 16:19, :] = jnp.where(slot == 0, tail[:3], tail[4:7])
        return carry

    lax.fori_loop(0, out_ref.shape[0], place, 0)


def body(nb, nc, f_home, levels, plan):
    devices = nb * nc
    patches = f_home.shape[0]
    target = plan // patches
    order = jnp.arange(patches, dtype=jnp.int32)
    earlier = (target[:, None] == target[None, :]) & (order[None, :] < order[:, None])
    place = 2 * target + jnp.sum(earlier.astype(jnp.int32), axis=1)
    hit = place[None, :] == jnp.arange(2 * devices, dtype=jnp.int32)[:, None]
    sidx = jnp.sum(jnp.where(hit, order[None, :], 0), axis=1)
    slot_of = jnp.sum(jnp.where(hit, plan[None, :] % patches + 1, 0), axis=1) - 1
    meta = jnp.broadcast_to(
        slot_of.astype(jnp.float32).reshape(devices, 2, 1), (devices, 2, CELLS)
    )
    lev = jnp.broadcast_to(
        levels.astype(jnp.float32).reshape(SPAN_PATCHES, DEPTH_PATCHES, 1),
        (SPAN_PATCHES, DEPTH_PATCHES, LANES),
    )
    vmem = pl.BlockSpec(memory_space=pltpu.VMEM)
    smem = pl.BlockSpec(memory_space=pltpu.SMEM)
    state = (19, SPAN_PATCHES, 8, CELLS)
    f32 = jnp.float32
    packed = pl.pallas_call(
        lambda *refs: lattice_kernel(nb, nc, *refs),
        out_shape=jax.ShapeDtypeStruct((devices, PACK, CELLS), f32),
        in_specs=[smem, vmem, vmem, vmem],
        out_specs=vmem,
        scratch_shapes=[
            pltpu.VMEM(state, f32),
            pltpu.VMEM(state, f32),
            pltpu.VMEM((18,) + state[1:], f32),
            pltpu.VMEM((patches, 19, CELLS), f32),
            pltpu.VMEM((len(AROUND), SPAN_PATCHES, 8, LANES), f32),
            pltpu.VMEM((STEPS, 2, 5, 8, CELLS), f32),
            pltpu.VMEM((STEPS, 2, 5, 8, CELLS), f32),
            pltpu.VMEM((STEPS, 2, 5, 2, 8, LANES), f32),
            pltpu.VMEM((STEPS, 2, 5, 2, 8, LANES), f32),
            pltpu.SemaphoreType.DMA((STEPS, 4)),
            pltpu.SemaphoreType.DMA((STEPS, 4)),
            pltpu.SemaphoreType.DMA((len(AROUND),)),
            pltpu.SemaphoreType.DMA((len(AROUND),)),
        ],
        compiler_params=pltpu.CompilerParams(collective_id=0, has_side_effects=True,
                                             vmem_limit_bytes=60 * 1024 * 1024),
    )(sidx, f_home, lev, meta)
    got = lax.all_to_all(packed, ("blocks", "cross"), split_axis=0, concat_axis=0, tiled=True)
    marks = jnp.stack([got[:, 35, 0], got[:, 39, 0]], axis=1).reshape(-1)
    match = marks[None, :] == jnp.arange(patches, dtype=f32)[:, None]
    ridx = jnp.sum(
        jnp.where(match, jnp.arange(2 * devices, dtype=jnp.int32)[None, :], 0), axis=1
    )
    return pl.pallas_call(
        unpack_kernel,
        out_shape=jax.ShapeDtypeStruct((patches, 19, CELLS), f32),
        in_specs=[smem, vmem],
        out_specs=vmem,
        compiler_params=pltpu.CompilerParams(vmem_limit_bytes=40 * 1024 * 1024),
    )(ridx, got)


def solution(mesh):
    nb, nc = mesh.shape["blocks"], mesh.shape["cross"]
    in_specs = (P(("blocks", "cross"), None, None), P(("blocks", "cross")), P(("blocks", "cross")))
    out_specs = P(("blocks", "cross"), None, None)
    return jax.shard_map(
        lambda f, l, p: body(nb, nc, f, l, p),
        mesh=mesh, in_specs=in_specs, out_specs=out_specs, check_vma=False)
```

time: 1200 us -> 110 us (0.09); the launches traced: 1180 us -> 110 us
  local copies, waits for them, and re-layouts: 919 us -> 7.05 us
  other arithmetic: 137 us -> 2.28 us
  waiting for transfers between devices: 94.6 us -> 0 us
  blocking collectives: 0 us -> 66 us
  Pallas kernels: 0 us -> 34.3 us
  starting transfers between devices: 23.6 us -> 0 us
    gather x70 -> x0, local copies, waits for them, and re-layouts: 190 us -> none  [the longest x23 55.4 us: face_payload(): balance[:, list(FACE_SPEEDS[face_id])]]
    slice x61 -> x1, local copies, waits for them, and re-layouts: 170 us -> 0.32 us  [body(): marks = jnp.stack([got[:, 35, 0], got[:, 39, 0]], axis=1).reshape(-1)]
    unnamed x379 -> x1, local copies, waits for them, and re-layouts: 150 us -> 3.18 us
    scatter x125 -> x0, local copies, waits for them, and re-layouts: 142 us -> none  [the longest x20 35.5 us: propagate(): padded.at[:, speed, 1:extent + 1, 1:extent + 1, 0]]
    reshape x7 -> x0, local copies, waits for them, and re-layouts: 79.4 us -> none  [the longest x2 55.4 us: home_ghosts(): extended = extended.reshape(extended.shape[:3] + (2, 6, 5, EDGE, EDGE))]
    squeeze x25 -> x0, local copies, waits for them, and re-layouts: 70.5 us -> none  [the longest x24 48.1 us: neighbour(): return eq_ext[window] + factor * neq_ext[window]]
    all_to_all x0 -> x1, blocking collectives: none -> 66 us  [body(): lax.all_to_all(packed, ('blocks', 'cross'), split_axis=0, concat_axis=0,...]
    another operation x50 -> x1, local copies, waits for them, and re-layouts: 62.7 us -> 0.09 us  [body(): marks = jnp.stack([got[:, 35, 0], got[:, 39, 0]], axis=1).reshape(-1)]
  transfers between devices with their start and end apart: 10 -> 0, of which waited for: 5 -> 0; matrix products, arithmetic and copies ran while one was open for 39% -> 0% of each run, Pallas kernels for 0% -> 0%
where the time goes in v1:
time: 110 us
  blocking collectives  66 us (60%)
  Pallas kernels  34.3 us (31%)
  local copies, waits for them, and re-layouts  7.05 us (6%)
  other arithmetic  2.28 us (2%)
    all_to_all x1, blocking collectives, body(): lax.all_to_all(packed, ('blocks', 'cross'), split_axis=0, concat_axis=0,...  66 us
    pallas_call x1, Pallas kernels, body(): pl.pallas_call(lambda *refs: lattice_kernel(nb, nc, *refs), out_shape=jax...  33.2 us
    unnamed x1, local copies, waits for them, and re-layouts  3.18 us

profile of v1, /device:TPU:0, one launch (start us, length us, event | category | flops | bytes accessed | tf_op | source)
XLA Modules:
  0.0 109.7 jit_solution(14625083942510131997)
XLA Ops:
  0.0 0.7 convert_element_type.17
  0.7 0.7 and_select_fusion.1
  1.3 0.2 convert_reduce_fusion
  1.5 0.6 select_reduce_fusion.1
  2.2 0.1 broadcast_in_dim.54
  2.2 0.1 convert_element_type.19
  2.3 3.2 %copy.10.refs_1_ = f32[32,19,512]{2,1,0:T(8,128)} copy(f32[32,19,512]{2,0,1:T(8,128)} %param.3) | data formatting | bytes 2490368 | tf_op args[0]
  5.5 0.7 broadcast_in_dim.55.refs_2_
  6.2 0.8 broadcast_in_dim.57.refs_3_
  6.9 33.2 %shard_map.37 = f32[32,40,512]{2,1,0:T(8,128)} custom-call(s32[64]{0:T(128)} %get-tuple-element.8.refs_0_, f32[32,19,512]{2,1,0:T(8,128)} %copy.10.refs_1_, f32[4,8,128]{2,1,0:T(8,128)} %broadcast_in_dim.55.refs_2_, f32[32,2,512]{2,1,0:T(2,128)} %broadcast_in_dim.57.refs_3_), custom_call_target="tpu_custom_call" | custom-call | tf_op jit(solution)/shard_map/pallas_call | solution.py:312
  40.1 66.0 %all_to_all.5.got_ref = f32[32,40,512]{2,1,0:T(8,128)S(1)} all-to-all(f32[32,40,512]{2,1,0:T(8,128)} %shard_map.37), channel_id=1, replica_groups=mesh['blocks'=16,'cross'=2] {'blocks','cross'}, dimensions={0} | all-to-all | bytes 5242880 | tf_op jit(solution)/shard_map/all_to_all | solution.py:335
  106.1 0.3 slice_reduce_fusion.1
  106.5 0.1 copy.11
  106.6 0.1 eq.49
  106.7 0.1 select_reduce_fusion.ridx
  106.8 1.1 shard_map.38
  107.9 1.8 %copy.12 = f32[32,19,512]{2,0,1:T(8,128)} copy(f32[32,19,512]{2,1,0:T(8,128)S(1)} %shard_map.38) | data formatting | bytes 2490368 | tf_op jit(solution)/shard_map/pallas_call | solution.py:341
  (3 shorter events, 0.0 us)

commit v2 on v1

--- a/solution.py
+++ b/solution.py
@@ -36,7 +36,9 @@
 RESCALE = TAU_FINE / (2.0 * TAU_COARSE)
 INFLOW = 0.08
 MESH = pl.DeviceIdType.MESH
-PACK = 40
+ROWS = 152
+MAIN = 16
+TAIL = 3
 LANES = 128
 TILES = CELLS // LANES
 Y_UP = [q for q in range(19) if VELOCITIES[q][1] == 1]
@@ -74,18 +76,56 @@
         store(q, balance + coef(q) * (f[q] - balance))
 
 
-def lattice_kernel(nb, nc, sidx, f_ref, lev_ref, meta_ref, out_ref, st, pb, cq, pm, lv, ys, yr, xs, xr,
-                   send_sem, recv_sem, lsend, lrecv):
+def lattice_kernel(nb, nc, sidx, slot_of, level, f_ref, got_ref, mark_ref, st, pb, cq, pm, sent, marks,
+                   lev_ref, lv, ys, yr, xs, xr, send_sem, recv_sem, lsend, lrecv, psend, precv,
+                   msend, mrecv):
+    others = nb * nc - 1
+    side = nb * nc // 2
     b = lax.axis_index("blocks")
     c = lax.axis_index("cross")
 
     def at(dx, dy):
         return (lax.rem(b + dx + nb, nb), lax.rem(c + dy + nc, nc))
 
+    me = b * nc + c
+    home_half = me // side
+    rank = lax.rem(me, side)
+
+    def peer(k):
+        far = (1 - home_half) * side + lax.rem(rank + k, side)
+        near = home_half * side + lax.rem(rank + 1 + k, side)
+        return jnp.where(k < side, far, near)
+
+    def device(d):
+        return (d // nc, lax.rem(d, nc))
+
     barrier = pltpu.get_barrier_semaphore()
-    for dx, dy in AROUND:
-        pl.semaphore_signal(barrier, inc=1, device_id=at(dx, dy), device_id_type=MESH)
-    pl.semaphore_wait(barrier, len(AROUND))
+
+    def greet(k, carry):
+        pl.semaphore_signal(barrier, inc=1, device_id=device(peer(k)), device_id_type=MESH)
+        return carry
+
+    lax.fori_loop(0, others, greet, 0)
+
+    spot = lax.broadcasted_iota(jnp.int32, (SPAN_PATCHES, 8, LANES), 0) * 8
+    spot = spot + lax.broadcasted_iota(jnp.int32, (SPAN_PATCHES, 8, LANES), 1)
+    own = jnp.zeros((SPAN_PATCHES, 8, LANES), jnp.float32)
+    for p in range(SPAN_PATCHES * 8):
+        own = jnp.where(spot == p, level[p].astype(jnp.float32), own)
+    lev_ref[...] = own
+
+    def note(d, carry):
+        row = lax.broadcasted_iota(jnp.int32, (8, LANES), 0)
+        first = slot_of[2 * d].astype(jnp.float32)
+        second = slot_of[2 * d + 1].astype(jnp.float32)
+        marks[d] = jnp.where(row == 0, first, second)
+        return carry
+
+    lax.fori_loop(0, others + 1, note, 0)
+    for q in range(19):
+        for r in range(SPAN_PATCHES):
+            st[q, r] = f_ref[q, r * 8 : r * 8 + 8, :]
+    pl.semaphore_wait(barrier, others)
 
     level_copies = []
     for n, (dx, dy) in enumerate(AROUND):
@@ -95,14 +135,28 @@
         copy.start()
         level_copies.append(copy)
 
-    for q in range(19):
-        for r in range(SPAN_PATCHES):
-            st[q, r] = f_ref[r * 8 : r * 8 + 8, q, :]
+    def mark_copy(k):
+        d = peer(k)
+        return pltpu.make_async_remote_copy(
+            src_ref=marks.at[d], dst_ref=mark_ref.at[me], send_sem=msend.at[k],
+            recv_sem=mrecv.at[k], device_id=device(d), device_id_type=MESH)
+
+    def patch_copy(k):
+        d = peer(k)
+        return pltpu.make_async_remote_copy(
+            src_ref=sent.at[d], dst_ref=got_ref.at[me], send_sem=psend.at[k],
+            recv_sem=precv.at[k], device_id=device(d), device_id_type=MESH)
+
+    def start_mark(k, carry):
+        mark_copy(k).start()
+        return carry
+
+    lax.fori_loop(0, others, start_mark, 0)
+    mark_ref[me] = marks[me]
 
     for copy in level_copies:
         copy.wait()
 
-    own = lev_ref[...]
     scale = {(0, 0): jnp.where(own > 0.5, RESCALE, 1.0)}
     for n, key in enumerate(AROUND):
         scale[key] = jnp.where(lv[n] > 0.5, RESCALE, 1.0)
@@ -185,31 +239,42 @@
         st[0] = pb[0]
         st[5] = pb[5]
         st[6] = pb[6]
+        def shift_x(wanted):
+            for way, e, group in ((0, 1, X_UP), (1, -1, X_DOWN)):
+                for n, q in enumerate(group):
+                    if (VELOCITIES[q][1] != 0) != wanted:
+                        continue
+                    v = roll(pb[q], 64 * e)
+                    pb[q] = v
+                    edge = v[:, :, :LANES] if e == 1 else v[:, :, CELLS - LANES :]
+                    turned = pltpu.roll(edge, 64, axis=2)
+                    if e == 1:
+                        xs[s, way, n] = jnp.where(half, edge[:2], turned[2:])
+                    else:
+                        xs[s, way, n] = jnp.where(half, turned[:2], edge[2:])
+
+        def shift_y(wanted):
+            for way, e, group in ((0, 1, Y_UP), (1, -1, Y_DOWN)):
+                for n, q in enumerate(group):
+                    if (VELOCITIES[q][0] != 0) != wanted:
+                        continue
+                    v = pb[q]
+                    halo = yr[s, way, n][None]
+                    if e == 1:
+                        moved = jnp.concatenate([halo, v[:-1]], axis=0)
+                    else:
+                        moved = jnp.concatenate([v[1:], halo], axis=0)
+                    v = jnp.where(entry[1, e], roll(moved, 8 * e - 64 * e), roll(v, 8 * e))
+                    if wanted:
+                        pb[q] = v
+                    else:
+                        st[q] = v
+
+        shift_x(False)
         for copy in y_copies:
             copy.wait()
-        for way, e, group in ((0, 1, Y_UP), (1, -1, Y_DOWN)):
-            for n, q in enumerate(group):
-                v = pb[q]
-                halo = yr[s, way, n][None]
-                if e == 1:
-                    moved = jnp.concatenate([halo, v[:-1]], axis=0)
-                else:
-                    moved = jnp.concatenate([v[1:], halo], axis=0)
-                v = jnp.where(entry[1, e], roll(moved, 8 * e - 64 * e), roll(v, 8 * e))
-                if VELOCITIES[q][0]:
-                    pb[q] = v
-                else:
-                    st[q] = v
-        for way, e, group in ((0, 1, X_UP), (1, -1, X_DOWN)):
-            for n, q in enumerate(group):
-                v = roll(pb[q], 64 * e)
-                pb[q] = v
-                edge = v[:, :, :LANES] if e == 1 else v[:, :, CELLS - LANES :]
-                turned = pltpu.roll(edge, 64, axis=2)
-                if e == 1:
-                    xs[s, way, n] = jnp.where(half, edge[:2], turned[2:])
-                else:
-                    xs[s, way, n] = jnp.where(half, turned[:2], edge[2:])
+        shift_y(True)
+        shift_x(True)
         x_copies = []
         for way, dx in ((0, 1), (1, -1)):
             copy = pltpu.make_async_remote_copy(
@@ -217,6 +282,7 @@
                 recv_sem=recv_sem.at[s, 2 + way], device_id=at(dx, 0), device_id_type=MESH)
             copy.start()
             x_copies.append(copy)
+        shift_y(False)
         for copy in x_copies:
             copy.wait()
         for way, e, group in ((0, 1, X_UP), (1, -1, X_DOWN)):
@@ -264,15 +330,36 @@
         for r in range(SPAN_PATCHES):
             pm[r * 8 : r * 8 + 8, q, :] = st[q, r]
 
-    def fill(d, carry):
+    def pack(d):
         for slot in range(2):
             p = sidx[2 * d + slot]
-            out_ref[d, 16 * slot : 16 * slot + 16, :] = pm[p, :16, :]
-            out_ref[d, 32 + 4 * slot : 35 + 4 * slot, :] = pm[p, 16:19, :]
-            out_ref[d, 35 + 4 * slot, :] = meta_ref[d, slot, :]
-        return carry
-
-    lax.fori_loop(0, nb * nc, fill, 0)
+            for tile in range(TILES):
+                lanes = slice(tile * LANES, (tile + 1) * LANES)
+                at_row = slot * TILES + tile
+                sent[d, at_row * MAIN : (at_row + 1) * MAIN, :] = pm[p, :MAIN, lanes]
+                low = 2 * TILES * MAIN + at_row * TAIL
+                sent[d, low : low + TAIL, :] = pm[p, MAIN:, lanes]
+
+    def post(k, carry):
+        pack(peer(k))
+
+        @pl.when(k > 0)
+        def _():
+            patch_copy(k - 1).start()
+
+        return carry
+
+    lax.fori_loop(0, others, post, 0)
+    pack(me)
+    patch_copy(others - 1).start()
+    got_ref[me] = sent[me]
+
+    def finish(k, carry):
+        mark_copy(k).wait()
+        patch_copy(k).wait()
+        return carry
+
+    lax.fori_loop(0, others, finish, 0)
 
 
 def unpack_kernel(ridx, got_ref, out_ref):
@@ -280,12 +367,20 @@
         a = ridx[t]
         src = a // 2
         slot = lax.rem(a, 2)
-        out_ref[t, :16, :] = got_ref[src, pl.ds(pl.multiple_of(slot * 16, 16), 16), :]
-        tail = got_ref[src, 32:40, :]
-        out_ref[t, 16:19, :] = jnp.where(slot == 0, tail[:3], tail[4:7])
-        return carry
-
-    lax.fori_loop(0, out_ref.shape[0], place, 0)
+        tail = got_ref[src, 2 * TILES * MAIN : ROWS, :]
+        for tile in range(TILES):
+            lanes = slice(tile * LANES, (tile + 1) * LANES)
+            low = pl.multiple_of((slot * TILES + tile) * MAIN, MAIN)
+            out_ref[:MAIN, t, lanes] = got_ref[src, pl.ds(low, MAIN), :]
+            other = TAIL * (TILES + tile)
+            rest = jnp.where(
+                slot == 0, tail[TAIL * tile : TAIL * (tile + 1)], tail[other : other + TAIL]
+            )
+            out_ref[MAIN:, t, lanes] = rest
+        return carry
+
+    for t in range(out_ref.shape[1]):
+        place(t, 0)
 
 
 def body(nb, nc, f_home, levels, plan):
@@ -298,53 +393,57 @@
     hit = place[None, :] == jnp.arange(2 * devices, dtype=jnp.int32)[:, None]
     sidx = jnp.sum(jnp.where(hit, order[None, :], 0), axis=1)
     slot_of = jnp.sum(jnp.where(hit, plan[None, :] % patches + 1, 0), axis=1) - 1
-    meta = jnp.broadcast_to(
-        slot_of.astype(jnp.float32).reshape(devices, 2, 1), (devices, 2, CELLS)
-    )
-    lev = jnp.broadcast_to(
-        levels.astype(jnp.float32).reshape(SPAN_PATCHES, DEPTH_PATCHES, 1),
-        (SPAN_PATCHES, DEPTH_PATCHES, LANES),
-    )
     vmem = pl.BlockSpec(memory_space=pltpu.VMEM)
     smem = pl.BlockSpec(memory_space=pltpu.SMEM)
     state = (19, SPAN_PATCHES, 8, CELLS)
+    small = (SPAN_PATCHES, 8, LANES)
     f32 = jnp.float32
-    packed = pl.pallas_call(
+    dma = pltpu.SemaphoreType.DMA
+    got, marks = pl.pallas_call(
         lambda *refs: lattice_kernel(nb, nc, *refs),
-        out_shape=jax.ShapeDtypeStruct((devices, PACK, CELLS), f32),
-        in_specs=[smem, vmem, vmem, vmem],
-        out_specs=vmem,
+        out_shape=(
+            jax.ShapeDtypeStruct((devices, ROWS, LANES), f32),
+            jax.ShapeDtypeStruct((devices, 8, LANES), f32),
+        ),
+        in_specs=[smem, smem, smem, vmem],
+        out_specs=(vmem, vmem),
         scratch_shapes=[
             pltpu.VMEM(state, f32),
             pltpu.VMEM(state, f32),
             pltpu.VMEM((18,) + state[1:], f32),
             pltpu.VMEM((patches, 19, CELLS), f32),
-            pltpu.VMEM((len(AROUND), SPAN_PATCHES, 8, LANES), f32),
+            pltpu.VMEM((devices, ROWS, LANES), f32),
+            pltpu.VMEM((devices, 8, LANES), f32),
+            pltpu.VMEM(small, f32),
+            pltpu.VMEM((len(AROUND),) + small, f32),
             pltpu.VMEM((STEPS, 2, 5, 8, CELLS), f32),
             pltpu.VMEM((STEPS, 2, 5, 8, CELLS), f32),
             pltpu.VMEM((STEPS, 2, 5, 2, 8, LANES), f32),
             pltpu.VMEM((STEPS, 2, 5, 2, 8, LANES), f32),
-            pltpu.SemaphoreType.DMA((STEPS, 4)),
-            pltpu.SemaphoreType.DMA((STEPS, 4)),
-            pltpu.SemaphoreType.DMA((len(AROUND),)),
-            pltpu.SemaphoreType.DMA((len(AROUND),)),
+            dma((STEPS, 4)),
+            dma((STEPS, 4)),
+            dma((len(AROUND),)),
+            dma((len(AROUND),)),
+            dma((devices - 1,)),
+            dma((devices - 1,)),
+            dma((devices - 1,)),
+            dma((devices - 1,)),
         ],
         compiler_params=pltpu.CompilerParams(collective_id=0, has_side_effects=True,
                                              vmem_limit_bytes=60 * 1024 * 1024),
-    )(sidx, f_home, lev, meta)
-    got = lax.all_to_all(packed, ("blocks", "cross"), split_axis=0, concat_axis=0, tiled=True)
-    marks = jnp.stack([got[:, 35, 0], got[:, 39, 0]], axis=1).reshape(-1)
-    match = marks[None, :] == jnp.arange(patches, dtype=f32)[:, None]
+    )(sidx, slot_of, levels, jnp.transpose(f_home, (1, 0, 2)))
+    match = marks[:, :2, 0].reshape(-1)[None, :] == jnp.arange(patches, dtype=f32)[:, None]
     ridx = jnp.sum(
         jnp.where(match, jnp.arange(2 * devices, dtype=jnp.int32)[None, :], 0), axis=1
     )
-    return pl.pallas_call(
+    out = pl.pallas_call(
         unpack_kernel,
-        out_shape=jax.ShapeDtypeStruct((patches, 19, CELLS), f32),
+        out_shape=jax.ShapeDtypeStruct((19, patches, CELLS), f32),
         in_specs=[smem, vmem],
         out_specs=vmem,
         compiler_params=pltpu.CompilerParams(vmem_limit_bytes=40 * 1024 * 1024),
     )(ridx, got)
+    return jnp.transpose(out, (1, 0, 2))
 
 
 def solution(mesh):

time: 110 us -> 98 us (0.89)
  blocking collectives: 66 us -> 0 us
  Pallas kernels: 34.3 us -> 92.4 us
  local copies, waits for them, and re-layouts: 7.05 us -> 2.82 us
    all_to_all x1 -> x0, blocking collectives: 66 us -> none  [body(): lax.all_to_all(packed, ('blocks', 'cross'), split_axis=0, concat_axis=0,...]
    pallas_call x2, Pallas kernels: 34.3 us -> 92.4 us  [the longest x1 89.9 us: body(): pl.pallas_call(lambda *refs: lattice_kernel(nb, nc, *refs), out_shape=(ja...]
    pallas_call x1 -> x0, local copies, waits for them, and re-layouts: 1.76 us -> none  [body(): pl.pallas_call(unpack_kernel, out_shape=jax.ShapeDtypeStruct((patches, 19...]
    broadcast_in_dim x3 -> x0, local copies, waits for them, and re-layouts: 1.5 us -> none  [the longest x1 0.76 us: body(): jnp.broadcast_to(slot_of.astype(jnp.float32).reshape(devices, 2, 1), (dev...]
    unnamed x1 -> x2, local copies, waits for them, and re-layouts: 3.18 us -> 1.7 us
where the time goes in v2:
time: 98 us; the launch traced here: 97.4 us
  Pallas kernels  92.4 us (94%)
  local copies, waits for them, and re-layouts  2.82 us (3%)
  other arithmetic  2.1 us (2%)
    pallas_call x1, Pallas kernels, body(): pl.pallas_call(lambda *refs: lattice_kernel(nb, nc, *refs), out_shape=(ja...  89.9 us
    pallas_call x1, Pallas kernels, body(): pl.pallas_call(unpack_kernel, out_shape=jax.ShapeDtypeStruct((19, patches...  2.55 us

profile of v2, /device:TPU:0, one launch (start us, length us, event | category | flops | bytes accessed | tf_op | source)
XLA Modules:
  0.0 97.4 jit_solution(8104537698923707504)
XLA Ops:
  0.0 0.7 and_select_fusion.1
  0.7 0.2 convert_reduce_fusion
  0.9 0.6 select_reduce_fusion.1
  1.5 0.5 broadcast_add_fusion.refs_1_
  2.0 89.9 %shard_map.37 = (f32[32,152,128]{2,1,0:T(8,128)}, f32[32,8,128]{2,1,0:T(8,128)}) custom-call(s32[64]{0:T(128)} %get-tuple-element.10.refs_0_, s32[64]{0:T(128)} %broadcast_add_fusion.refs_1_, s32[32]{0:T(128)} %refs_2_.1, f32[19,32,512]{2,1,0:T(8,128)} %bitcast.2), custom_call_target="tpu_custom_call" | custom-call | tf_op jit(solution)/shard_map/pallas_call | solution.py:402
  91.9 1.0 %slice_reduce_fusion = f32[32,2]{1,0:T(8,128)S(1)} fusion(f32[32,8,128]{2,1,0:T(8,128)} %get-tuple-element.7), kind=kLoop, calls=%fused_computation | loop fusion | bytes 512 | tf_op jit(solution)/shard_map/slice | solution.py:435
  92.9 0.1 eq.49
  93.0 0.1 select_reduce_fusion.ridx
  93.1 0.0 copy-start
  93.1 1.7 %copy-done = f32[32,152,128]{2,1,0:T(8,128)S(1)} copy-done((f32[32,152,128]{2,1,0:T(8,128)S(1)}, f32[32,152,128]{2,1,0:T(8,128)}, u32[]{:S(2)}) %copy-start) | copy-done | bytes 2490392
  94.8 2.5 %shard_map.38 = f32[19,32,512]{2,1,0:T(8,128)} custom-call(s32[32]{0:T(128)S(1)} %select_reduce_fusion.ridx, f32[32,152,128]{2,1,0:T(8,128)S(1)} %copy-done), custom_call_target="tpu_custom_call" | custom-call | tf_op jit(solution)/shard_map/pallas_call | solution.py:439
  (1 shorter events, 0.0 us)
Async XLA Ops:
  93.1 1.7 %copy-start = (f32[32,152,128]{2,1,0:T(8,128)S(1)}, f32[32,152,128]{2,1,0:T(8,128)}, u32[]{:S(2)}) copy-start(f32[32,152,128]{2,1,0:T(8,128)} %get-tuple-element.8.got_ref) | copy-start | bytes 7471108

commit v3 on v2

--- a/solution.py
+++ b/solution.py
@@ -50,18 +50,18 @@
 
 def relax_into(load, store, coef):
     f = [load(q) for q in range(19)]
-    rho = f[0]
-    for q in range(1, 19):
-        rho = rho + f[q]
+    terms = list(f)
+    while len(terms) > 1:
+        pairs = [a + b for a, b in zip(terms[::2], terms[1::2])]
+        terms = pairs + ([terms[-1]] if len(terms) % 2 else [])
+    rho = terms[0]
     inv = 1.0 / rho
     u = []
     for axis in range(3):
         up = [f[q] for q in range(19) if VELOCITIES[q][axis] == 1]
         down = [f[q] for q in range(19) if VELOCITIES[q][axis] == -1]
-        total = up[0] - down[0]
-        for a, b in zip(up[1:], down[1:]):
-            total = total + (a - b)
-        u.append(total * inv)
+        d = [a - b for a, b in zip(up, down)]
+        u.append((((d[0] + d[1]) + (d[2] + d[3])) + d[4]) * inv)
     base = 1.0 - 1.5 * (u[0] * u[0] + u[1] * u[1] + u[2] * u[2])
     scaled = {w: w * rho for w in set(WEIGHTS)}
     for q in range(19):
@@ -76,7 +76,7 @@
         store(q, balance + coef(q) * (f[q] - balance))
 
 
-def lattice_kernel(nb, nc, sidx, slot_of, level, f_ref, got_ref, mark_ref, st, pb, cq, pm, sent, marks,
+def lattice_kernel(nb, nc, sidx, slot_of, level, f_ref, got_ref, table_ref, st, pb, cq, pm, sent, marks, mark_ref,
                    lev_ref, lv, ys, yr, xs, xr, send_sem, recv_sem, lsend, lrecv, psend, precv,
                    msend, mrecv):
     others = nb * nc - 1
@@ -206,9 +206,8 @@
         return pltpu.roll(v, amount % CELLS, axis=2)
 
     def step(s, carry):
-        def chunk(t, carry):
-            r = t // TILES
-            lanes = pl.ds(pl.multiple_of(lax.rem(t, TILES) * LANES, LANES), LANES)
+        def first(r, tile):
+            lanes = slice(tile * LANES, (tile + 1) * LANES)
             plain = jnp.where(lev_ref[r] > 0.5, 1.0 - 1.0 / TAU_FINE, 1.0 - 1.0 / TAU_COARSE)
 
             def put(q, value):
@@ -216,16 +215,23 @@
 
             relax_into(lambda q: st[q, r, :, lanes], put,
                        lambda q: cq[q - 1, r, :, lanes] if q else plain)
-            return carry
-
-        lax.fori_loop(0, SPAN_PATCHES * TILES, chunk, 0)
-
-        for q in range(19):
+
+        def shift_z(q, rows):
             e = VELOCITIES[q][2]
             if e:
-                v = pb[q]
+                v = pb[q, rows]
                 wrapped = pltpu.roll(roll(v, e - 8 * e), e % 8, axis=1)
-                pb[q] = jnp.where(entry[2, e], wrapped, roll(v, e))
+                pb[q, rows] = jnp.where(entry[2, e][rows], wrapped, roll(v, e))
+
+        def outer(m, carry):
+            for tile in range(TILES):
+                first(m * (SPAN_PATCHES - 1), tile)
+            return carry
+
+        lax.fori_loop(0, 2, outer, 0)
+        for r in (0, SPAN_PATCHES - 1):
+            for q in range(19):
+                shift_z(q, slice(r, r + 1))
         for n in range(5):
             ys[s, 0, n] = pb[Y_UP[n], SPAN_PATCHES - 1]
             ys[s, 1, n] = pb[Y_DOWN[n], 0]
@@ -236,6 +242,15 @@
                 recv_sem=recv_sem.at[s, way], device_id=at(0, dy), device_id_type=MESH)
             copy.start()
             y_copies.append(copy)
+
+        def inner(r, carry):
+            for tile in range(TILES):
+                first(r, tile)
+            return carry
+
+        lax.fori_loop(1, SPAN_PATCHES - 1, inner, 0)
+        for q in range(19):
+            shift_z(q, slice(1, SPAN_PATCHES - 1))
         st[0] = pb[0]
         st[5] = pb[5]
         st[6] = pb[6]
@@ -283,6 +298,23 @@
             copy.start()
             x_copies.append(copy)
         shift_y(False)
+        for q in X_UP + X_DOWN:
+            st[q] = pb[q]
+
+        def again(r, tiles):
+            for tile in tiles:
+                lanes = slice(tile * LANES, (tile + 1) * LANES)
+
+                def put(q, value):
+                    pb[q, r, :, lanes] = value
+
+                relax_into(lambda q: st[q, r, :, lanes], put, lambda q: 1.0 - 1.0 / TAU_FINE)
+
+        def middle(r, carry):
+            again(r, range(1, TILES - 1))
+            return carry
+
+        lax.fori_loop(0, SPAN_PATCHES, middle, 0)
         for copy in x_copies:
             copy.wait()
         for way, e, group in ((0, 1, X_UP), (1, -1, X_DOWN)):
@@ -295,23 +327,15 @@
                 const = WEIGHTS[q] * (1.0 + 3.0 * along + 4.5 * along * along - 1.5 * INFLOW * INFLOW)
                 halo = jnp.where(outside, jnp.full(halo.shape, const, jnp.float32), halo)
                 if e == 1:
-                    st[q, :, :, LANES:] = pb[q, :, :, LANES:]
-                    st[q, :, :, :LANES] = jnp.where(lane < 64, halo, pb[q, :, :, :LANES])
+                    st[q, :, :, :LANES] = jnp.where(lane < 64, halo, st[q, :, :, :LANES])
                 else:
-                    st[q, :, :, : CELLS - LANES] = pb[q, :, :, : CELLS - LANES]
-                    st[q, :, :, CELLS - LANES :] = jnp.where(lane >= 64, halo, pb[q, :, :, CELLS - LANES :])
-
-        def again(t, carry):
-            r = t // TILES
-            lanes = pl.ds(pl.multiple_of(lax.rem(t, TILES) * LANES, LANES), LANES)
-
-            def put(q, value):
-                pb[q, r, :, lanes] = value
-
-            relax_into(lambda q: st[q, r, :, lanes], put, lambda q: 1.0 - 1.0 / TAU_FINE)
+                    st[q, :, :, CELLS - LANES :] = jnp.where(lane >= 64, halo, st[q, :, :, CELLS - LANES :])
+
+        def ends(r, carry):
+            again(r, (0, TILES - 1))
             return carry
 
-        lax.fori_loop(0, SPAN_PATCHES * TILES, again, 0)
+        lax.fori_loop(0, SPAN_PATCHES, ends, 0)
         for q in range(19):
             e = VELOCITIES[q]
             take = fine
@@ -354,8 +378,18 @@
     patch_copy(others - 1).start()
     got_ref[me] = sent[me]
 
+    def marked(k, carry):
+        mark_copy(k).wait()
+        return carry
+
+    lax.fori_loop(0, others, marked, 0)
+    source = lax.broadcasted_iota(jnp.int32, (others + 1, LANES), 0) * 2
+    wanted = lax.broadcasted_iota(jnp.int32, (others + 1, LANES), 1).astype(jnp.float32)
+    index = jnp.where(mark_ref[:, 0, :] == wanted, source, 0)
+    index = index + jnp.where(mark_ref[:, 1, :] == wanted, source + 1, 0)
+    table_ref[...] = jnp.broadcast_to(jnp.sum(index, axis=0, keepdims=True), (8, LANES))
+
     def finish(k, carry):
-        mark_copy(k).wait()
         patch_copy(k).wait()
         return carry
 
@@ -364,7 +398,7 @@
 
 def unpack_kernel(ridx, got_ref, out_ref):
     def place(t, carry):
-        a = ridx[t]
+        a = ridx[0, t]
         src = a // 2
         slot = lax.rem(a, 2)
         tail = got_ref[src, 2 * TILES * MAIN : ROWS, :]
@@ -399,11 +433,11 @@
     small = (SPAN_PATCHES, 8, LANES)
     f32 = jnp.float32
     dma = pltpu.SemaphoreType.DMA
-    got, marks = pl.pallas_call(
+    got, ridx = pl.pallas_call(
         lambda *refs: lattice_kernel(nb, nc, *refs),
         out_shape=(
             jax.ShapeDtypeStruct((devices, ROWS, LANES), f32),
-            jax.ShapeDtypeStruct((devices, 8, LANES), f32),
+            jax.ShapeDtypeStruct((8, LANES), jnp.int32),
         ),
         in_specs=[smem, smem, smem, vmem],
         out_specs=(vmem, vmem),
@@ -413,6 +447,7 @@
             pltpu.VMEM((18,) + state[1:], f32),
             pltpu.VMEM((patches, 19, CELLS), f32),
             pltpu.VMEM((devices, ROWS, LANES), f32),
+            pltpu.VMEM((devices, 8, LANES), f32),
             pltpu.VMEM((devices, 8, LANES), f32),
             pltpu.VMEM(small, f32),
             pltpu.VMEM((len(AROUND),) + small, f32),
@@ -432,10 +467,6 @@
         compiler_params=pltpu.CompilerParams(collective_id=0, has_side_effects=True,
                                              vmem_limit_bytes=60 * 1024 * 1024),
     )(sidx, slot_of, levels, jnp.transpose(f_home, (1, 0, 2)))
-    match = marks[:, :2, 0].reshape(-1)[None, :] == jnp.arange(patches, dtype=f32)[:, None]
-    ridx = jnp.sum(
-        jnp.where(match, jnp.arange(2 * devices, dtype=jnp.int32)[None, :], 0), axis=1
-    )
     out = pl.pallas_call(
         unpack_kernel,
         out_shape=jax.ShapeDtypeStruct((19, patches, CELLS), f32),

time: 98 us -> 94.4 us (0.963)
  Pallas kernels: 92.4 us -> 89.3 us
    pallas_call x1, Pallas kernels: 89.9 us -> 86.7 us  [body(): pl.pallas_call(lambda *refs: lattice_kernel(nb, nc, *refs), out_shape=(ja...]
    slice x1 -> x0, local copies, waits for them, and re-layouts: 1.01 us -> none  [body(): marks[:, :2, 0].reshape(-1)[None, :]]
    unnamed x2 -> x4, local copies, waits for them, and re-layouts: 1.7 us -> 2.38 us
where the time goes in v3:
time: 94.4 us; the launch traced here: 93.7 us
  Pallas kernels  89.3 us (95%)
  local copies, waits for them, and re-layouts  2.38 us (3%)
  other arithmetic  2.05 us (2%)
    pallas_call x1, Pallas kernels, body(): pl.pallas_call(lambda *refs: lattice_kernel(nb, nc, *refs), out_shape=(ja...  86.7 us
    pallas_call x1, Pallas kernels, body(): pl.pallas_call(unpack_kernel, out_shape=jax.ShapeDtypeStruct((19, patches...  2.61 us
    unnamed x4, local copies, waits for them, and re-layouts  2.38 us

profile of v3, /device:TPU:0, one launch (start us, length us, event | category | flops | bytes accessed | tf_op | source)
XLA Modules:
  0.0 93.7 jit_solution(12953955409429898238)
XLA Ops:
  0.0 0.7 and_select_fusion.1
  0.7 0.2 convert_reduce_fusion
  0.9 0.6 select_reduce_fusion
  1.5 0.6 broadcast_add_fusion.refs_1_
  2.1 86.7 %shard_map.37 = (f32[32,152,128]{2,1,0:T(8,128)}, s32[8,128]{1,0:T(8,128)}) custom-call(s32[64]{0:T(128)} %get-tuple-element.10.refs_0_, s32[64]{0:T(128)} %broadcast_add_fusion.refs_1_, s32[32]{0:T(128)} %refs_2_.1, f32[19,32,512]{2,1,0:T(8,128)} %bitcast.2), custom_call_target="tpu_custom_call" | custom-call | tf_op jit(solution)/shard_map/pallas_call | solution.py:436
  88.7 0.0 copy-start
  88.8 1.7 %copy-done = f32[32,152,128]{2,1,0:T(8,128)S(1)} copy-done((f32[32,152,128]{2,1,0:T(8,128)S(1)}, f32[32,152,128]{2,1,0:T(8,128)}, u32[]{:S(2)}) %copy-start) | copy-done | bytes 2490392
  90.4 0.0 copy-start.1
  90.4 0.7 copy-done.1
  91.1 2.6 %shard_map.38 = f32[19,32,512]{2,1,0:T(8,128)} custom-call(s32[8,128]{1,0:T(8,128)S(1)} %copy-done.1, f32[32,152,128]{2,1,0:T(8,128)S(1)} %copy-done), custom_call_target="tpu_custom_call" | custom-call | tf_op jit(solution)/shard_map/pallas_call | solution.py:470
  (1 shorter events, 0.0 us)
Async XLA Ops:
  88.7 1.7 %copy-start = (f32[32,152,128]{2,1,0:T(8,128)S(1)}, f32[32,152,128]{2,1,0:T(8,128)}, u32[]{:S(2)}) copy-start(f32[32,152,128]{2,1,0:T(8,128)} %get-tuple-element.8.got_ref) | copy-start | bytes 7471108
  90.4 0.7 copy-start.1

commit v4 on v3

--- a/solution.py
+++ b/solution.py
@@ -114,17 +114,6 @@
         own = jnp.where(spot == p, level[p].astype(jnp.float32), own)
     lev_ref[...] = own
 
-    def note(d, carry):
-        row = lax.broadcasted_iota(jnp.int32, (8, LANES), 0)
-        first = slot_of[2 * d].astype(jnp.float32)
-        second = slot_of[2 * d + 1].astype(jnp.float32)
-        marks[d] = jnp.where(row == 0, first, second)
-        return carry
-
-    lax.fori_loop(0, others + 1, note, 0)
-    for q in range(19):
-        for r in range(SPAN_PATCHES):
-            st[q, r] = f_ref[q, r * 8 : r * 8 + 8, :]
     pl.semaphore_wait(barrier, others)
 
     level_copies = []
@@ -135,6 +124,17 @@
         copy.start()
         level_copies.append(copy)
 
+    def note(d, carry):
+        row = lax.broadcasted_iota(jnp.int32, (8, LANES), 0)
+        first = slot_of[2 * d].astype(jnp.float32)
+        second = slot_of[2 * d + 1].astype(jnp.float32)
+        marks[d] = jnp.where(row == 0, first, second)
+        return carry
+
+    lax.fori_loop(0, others + 1, note, 0)
+    for q in range(19):
+        for r in range(SPAN_PATCHES):
+            st[q, r] = f_ref[q, r * 8 : r * 8 + 8, :]
     def mark_copy(k):
         d = peer(k)
         return pltpu.make_async_remote_copy(

time: 94.4 us -> 95.2 us (level)
  no operation moved by 1% of the time
where the time goes in v4:
time: 95.2 us; the launch traced here: 93.6 us
  Pallas kernels  89.1 us (94%)
  local copies, waits for them, and re-layouts  2.38 us (2%)
  other arithmetic  2.05 us (2%)
    pallas_call x1, Pallas kernels, body(): pl.pallas_call(lambda *refs: lattice_kernel(nb, nc, *refs), out_shape=(ja...  86.5 us
    pallas_call x1, Pallas kernels, body(): pl.pallas_call(unpack_kernel, out_shape=jax.ShapeDtypeStruct((19, patches...  2.61 us
    unnamed x4, local copies, waits for them, and re-layouts  2.38 us

profile of v4, /device:TPU:0, one launch (start us, length us, event | category | flops | bytes accessed | tf_op | source)
XLA Modules:
  0.0 93.6 jit_solution(1433043456288095162)
XLA Ops:
  0.0 0.7 and_select_fusion.1
  0.7 0.2 convert_reduce_fusion
  0.9 0.6 select_reduce_fusion
  1.5 0.6 broadcast_add_fusion.refs_1_
  2.1 86.5 %shard_map.37 = (f32[32,152,128]{2,1,0:T(8,128)}, s32[8,128]{1,0:T(8,128)}) custom-call(s32[64]{0:T(128)} %get-tuple-element.10.refs_0_, s32[64]{0:T(128)} %broadcast_add_fusion.refs_1_, s32[32]{0:T(128)} %refs_2_.1, f32[19,32,512]{2,1,0:T(8,128)} %bitcast.2), custom_call_target="tpu_custom_call" | custom-call | tf_op jit(solution)/shard_map/pallas_call | solution.py:436
  88.6 0.0 copy-start
  88.6 1.7 %copy-done = f32[32,152,128]{2,1,0:T(8,128)S(1)} copy-done((f32[32,152,128]{2,1,0:T(8,128)S(1)}, f32[32,152,128]{2,1,0:T(8,128)}, u32[]{:S(2)}) %copy-start) | copy-done | bytes 2490392
  90.3 0.0 copy-start.1
  90.3 0.7 copy-done.1
  91.0 2.6 %shard_map.38 = f32[19,32,512]{2,1,0:T(8,128)} custom-call(s32[8,128]{1,0:T(8,128)S(1)} %copy-done.1, f32[32,152,128]{2,1,0:T(8,128)S(1)} %copy-done), custom_call_target="tpu_custom_call" | custom-call | tf_op jit(solution)/shard_map/pallas_call | solution.py:470
  (1 shorter events, 0.0 us)
Async XLA Ops:
  88.6 1.7 %copy-start = (f32[32,152,128]{2,1,0:T(8,128)S(1)}, f32[32,152,128]{2,1,0:T(8,128)}, u32[]{:S(2)}) copy-start(f32[32,152,128]{2,1,0:T(8,128)} %get-tuple-element.8.got_ref) | copy-start | bytes 7471108
  90.3 0.7 copy-start.1
